TPU v7x, 64 devices: a 2x2x8 block of a 4x4x8 slice. The times are simulated.
64 devices in a mesh: rep: 4 (over x, y), dp: 16 (over z, core).
Axes of the slice: x: 2, y: 2, z: 8, core: 2. Of those that a mesh axis runs over, the one named last changes fastest.
The devices are a block of a 4x4x8 slice.
Arguments:
- g_w_gate: bfloat16 [64, 2, 768, 1792], P(('rep', 'dp')), parts along dimension 0
- g_w_up: bfloat16 [64, 2, 768, 1792], P(('rep', 'dp')), parts along dimension 0
- g_w_down: bfloat16 [64, 2, 1792, 768], P(('rep', 'dp')), parts along dimension 0
- w_gate: bfloat16 [2, 768, 1792], replicated
- w_up: bfloat16 [2, 768, 1792], replicated
- w_down: bfloat16 [2, 1792, 768], replicated
- m_w_gate: float32 [2, 768, 1792], P(None, 'dp')
- m_w_up: float32 [2, 768, 1792], P(None, 'dp')
- m_w_down: float32 [2, 1792, 768], P(None, 'dp')
- v_w_gate: float32 [2, 768, 1792], P(None, 'dp')
- v_w_up: float32 [2, 768, 1792], P(None, 'dp')
- v_w_down: float32 [2, 1792, 768], P(None, 'dp')
Outputs:
- output 1: bfloat16 [8, 768, 1792], P('rep'), parts along dimension 0
- output 2: bfloat16 [8, 768, 1792], P('rep'), parts along dimension 0
- output 3: bfloat16 [8, 1792, 768], P('rep'), parts along dimension 0
- output 4: float32 [8, 768, 1792], P('rep', 'dp'), parts along dimension 0
- output 5: float32 [8, 768, 1792], P('rep', 'dp'), parts along dimension 0
- output 6: float32 [8, 1792, 768], P('rep', 'dp'), parts along dimension 0
- output 7: float32 [8, 768, 1792], P('rep', 'dp'), parts along dimension 0
- output 8: float32 [8, 768, 1792], P('rep', 'dp'), parts along dimension 0
- output 9: float32 [8, 1792, 768], P('rep', 'dp'), parts along dimension 0
There are 4 independent parts. A program takes and returns all parts, laid end to end along the dimension named above; an argument that names none is the same for every part.
All inputs are finite; a program needn't handle non-finite values.
Results may differ from a plain program's by a relative error of at most 0.022.
Values are sent between devices in bfloat16 or wider.
A program may use at most 768 MiB of HBM per device.

v0:
```python
import jax
import jax.numpy as jnp
from jax import lax
from jax.sharding import PartitionSpec as P


def adamw(w, m, v, g):
    m = 0.9 * m + 0.1 * g
    v = 0.95 * v + 0.05 * g * g
    step = m * lax.rsqrt(v + 1e-8) + 0.1 * w
    return (w - 0.02 * step).astype(jnp.bfloat16), m, v


def solution(mesh):
    def step(*arrays):
        terms, weights, m, v = (arrays[i : i + 3] for i in (0, 3, 6, 9))
        gradients = [lax.psum_scatter(t[0], "dp", scatter_dimension=1, tiled=True).astype(jnp.float32) for t in terms]
        me = lax.axis_index("dp")
        own = [lax.dynamic_slice_in_dim(w, me * one.shape[1], one.shape[1], 1).astype(jnp.float32) for w, one in zip(weights, m, strict=True)]
        new = [adamw(w, m, v, g) for w, m, v, g in zip(own, m, v, gradients, strict=True)]
        whole = [lax.all_gather(one[0], "dp", axis=1, tiled=True) for one in new]
        return (*whole, *(one[1] for one in new), *(one[2] for one in new))

    all_of, cut = P(None, None, None), P(None, "dp", None)
    return jax.shard_map(
        step,
        mesh=mesh,
        in_specs=(P(("rep", "dp"), None, None, None),) * 3 + (all_of,) * 3 + (cut,) * 6,
        out_specs=(P("rep", None, None),) * 3 + (P("rep", "dp", None),) * 6,
        check_vma=False,
    )
```

profile of v0, /device:TPU:21, one launch (start us, length us, event | category | flops | bytes accessed | tf_op | source)
XLA Modules:
  0.0 347.3 jit_solution(17769804537438258312)
XLA Ops:
  7.2 0.1 reduce-scatter.8.cloned.1.call-start
  7.3 0.7 reduce-scatter.8.cloned.1.call-update
  8.0 0.1 reduce-scatter.6.cloned.1.call-start
  8.1 0.0 copy-start.1
  8.1 0.0 copy-start.2
  8.1 0.7 reduce-scatter.6.cloned.1.call-update
  8.8 0.0 copy-start.3
  8.8 0.0 copy-start.4
  8.8 0.1 reduce-scatter.4.cloned.1.call-start
  8.9 0.7 reduce-scatter.4.cloned.1.call-update
  9.6 0.0 copy-start.5
  9.6 0.1 all-gather.8.cloned.1.call-start
  9.7 64.5 %reduce-scatter.8.cloned.1.call-done = bf16[2,112,768]{2,1,0:T(8,128)(2,1)} async-done(((bf16[2,1792,768]{2,1,0:T(8,128)(2,1)}), bf16[2,112,768]{2,1,0:T(8,128)(2,1)}) %reduce-scatter.8.cloned.1.call-update) | async-done | bytes 344080 | tf_op jit(solution)/shard_map/reduce_scatter | solution.py:17
  74.2 0.0 copy-done.1
  74.2 0.0 copy-done.2
  74.2 2.4 fusion.10
  76.7 0.1 all-gather.8.cloned.1.call-update
  76.7 0.1 all-gather.6.cloned.1.call-start
  76.8 60.8 %reduce-scatter.6.cloned.1.call-done = bf16[2,48,1792]{2,1,0:T(8,128)(2,1)} async-done(((bf16[2,768,1792]{2,1,0:T(8,128)(2,1)}), bf16[2,48,1792]{2,1,0:T(8,128)(2,1)}) %reduce-scatter.6.cloned.1.call-update) | async-done | bytes 344080 | tf_op jit(solution)/shard_map/reduce_scatter | solution.py:17
  137.6 0.0 copy-done.3
  137.6 0.0 copy-done.4
  137.6 2.4 fusion.6
  140.0 0.1 all-gather.6.cloned.1.call-update
  140.1 0.1 all-gather.4.cloned.1.call-start
  140.2 60.7 %reduce-scatter.4.cloned.1.call-done = bf16[2,48,1792]{2,1,0:T(8,128)(2,1)} async-done(((bf16[2,768,1792]{2,1,0:T(8,128)(2,1)}), bf16[2,48,1792]{2,1,0:T(8,128)(2,1)}) %reduce-scatter.4.cloned.1.call-update) | async-done | bytes 344080 | tf_op jit(solution)/shard_map/reduce_scatter | solution.py:17
  200.9 0.0 copy-done.5
  200.9 2.6 fusion.2
  203.5 0.1 all-gather.4.cloned.1.call-update
  203.6 42.1 %all-gather.8.cloned.1.call-done = bf16[2,1792,768]{2,1,0:T(8,128)(2,1)} async-done(((bf16[2,112,768]{2,1,0:T(8,128)(2,1)}), bf16[2,1792,768]{2,1,0:T(8,128)(2,1)}) %all-gather.8.cloned.1.call-update) | async-done | bytes 5505040 | tf_op jit(solution)/shard_map/all_gather | solution.py:21
  245.7 41.2 %all-gather.6.cloned.1.call-done = bf16[2,768,1792]{2,1,0:T(8,128)(2,1)} async-done(((bf16[2,48,1792]{2,1,0:T(8,128)(2,1)}), bf16[2,768,1792]{2,1,0:T(8,128)(2,1)}) %all-gather.6.cloned.1.call-update) | async-done | bytes 5505040 | tf_op jit(solution)/shard_map/all_gather | solution.py:21
  286.9 41.2 %all-gather.4.cloned.1.call-done = bf16[2,768,1792]{2,1,0:T(8,128)(2,1)} async-done(((bf16[2,48,1792]{2,1,0:T(8,128)(2,1)}), bf16[2,768,1792]{2,1,0:T(8,128)(2,1)}) %all-gather.4.cloned.1.call-update) | async-done | bytes 5505040 | tf_op jit(solution)/shard_map/all_gather | solution.py:21
  328.1 0.0 copy-start
  328.1 0.0 slice-start
  328.1 5.9 %copy.24 = bf16[2,768,1792]{2,1,0:T(8,128)(2,1)} copy(bf16[2,768,1792]{2,1,0:T(8,128)(2,1)} %all-gather.4.cloned.1.call-done) | data formatting | bytes 11010048
  334.0 0.0 copy-done
  334.0 0.0 slice-start.1
  334.0 2.8 copy.25
  336.8 0.1 slice-done
  336.9 1.1 slice-done.1
  338.0 2.4 copy.26
  (1 shorter events, 0.0 us)
Async XLA Ops:
  7.2 67.0 %reduce-scatter.8.cloned.1.call-start = ((), (), s32[]{:S(2)}) async-start(), calls=%async_computation.7 | async-start | bytes 5849088 | tf_op jit(solution)/shard_map/reduce_scatter | solution.py:17
  8.0 129.6 %reduce-scatter.6.cloned.1.call-start = ((), (), s32[]{:S(2)}) async-start(), calls=%async_computation.5 | async-start | bytes 5849088 | tf_op jit(solution)/shard_map/reduce_scatter | solution.py:17
  8.1 66.2 %copy-start.1 = (f32[2,112,768]{2,1,0:T(8,128)S(1)}, f32[2,112,768]{2,1,0:T(8,128)}, u32[]{:S(2)}) copy-start(f32[2,112,768]{2,1,0:T(8,128)} %param.23) | copy-start | bytes 2064388
  8.1 66.2 %copy-start.2 = (f32[2,112,768]{2,1,0:T(8,128)S(1)}, f32[2,112,768]{2,1,0:T(8,128)}, u32[]{:S(2)}) copy-start(f32[2,112,768]{2,1,0:T(8,128)} %param.20) | copy-start | bytes 2064388
  8.8 128.8 %copy-start.3 = (f32[2,48,1792]{2,1,0:T(8,128)S(1)}, f32[2,48,1792]{2,1,0:T(8,128)}, u32[]{:S(2)}) copy-start(f32[2,48,1792]{2,1,0:T(8,128)} %param.22) | copy-start | bytes 2064388
  8.8 128.8 %copy-start.4 = (f32[2,48,1792]{2,1,0:T(8,128)S(1)}, f32[2,48,1792]{2,1,0:T(8,128)}, u32[]{:S(2)}) copy-start(f32[2,48,1792]{2,1,0:T(8,128)} %param.19) | copy-start | bytes 2064388
  8.8 192.1 %reduce-scatter.4.cloned.1.call-start = ((), (), s32[]{:S(2)}) async-start(), calls=%async_computation.3 | async-start | bytes 5849088 | tf_op jit(solution)/shard_map/reduce_scatter | solution.py:17
  9.6 191.3 %copy-start.5 = (f32[2,48,1792]{2,1,0:T(8,128)S(1)}, f32[2,48,1792]{2,1,0:T(8,128)}, u32[]{:S(2)}) copy-start(f32[2,48,1792]{2,1,0:T(8,128)} %param.21) | copy-start | bytes 2064388
  9.6 236.1 %all-gather.8.cloned.1.call-start = ((), (), s32[]{:S(2)}) async-start(), calls=%async_computation.8 | async-start | bytes 5849088 | tf_op jit(solution)/shard_map/all_gather | solution.py:21
  76.7 210.2 %all-gather.6.cloned.1.call-start = ((), (), s32[]{:S(2)}) async-start(), calls=%async_computation.6 | async-start | bytes 5849088 | tf_op jit(solution)/shard_map/all_gather | solution.py:21
  140.1 188.0 %all-gather.4.cloned.1.call-start = ((), (), s32[]{:S(2)}) async-start(), calls=%async_computation.4 | async-start | bytes 5849088 | tf_op jit(solution)/shard_map/all_gather | solution.py:21
  328.1 5.9 %copy-start = (bf16[2,768,1792]{2,1,0:T(8,128)(2,1)S(1)}, bf16[2,768,1792]{2,1,0:T(8,128)(2,1)}, u32[]{:S(2)}) copy-start(bf16[2,768,1792]{2,1,0:T(8,128)(2,1)} %all-gather.6.cloned.1.call-done) | copy-start | bytes 16515076
  328.1 8.8 %slice-start = ((s8[5505024]{0:T(1024)(128)(4,1)}), s8[4194304]{0:T(1024)(128)(4,1)S(1)}, s32[]{:S(2)}) async-start(s8[5505024]{0:T(1024)(128)(4,1)} %bitcast.3), calls=%async_computation.9 | async-start | bytes 8388608
  334.0 4.0 %slice-start.1 = ((s8[5505024]{0:T(1024)(128)(4,1)}), s8[1310720]{0:T(1024)(128)(4,1)S(1)}, s32[]{:S(2)}) async-start(s8[5505024]{0:T(1024)(128)(4,1)} %bitcast.3), calls=%async_computation.10 | async-start | bytes 2621440
Sparse Core Ops, SparseCore 0:
  10.4 63.7 reduce-scatter.7
  76.6 60.9 reduce-scatter.5
  140.0 60.8 reduce-scatter.3
  203.0 42.7 all-gather.7
  247.8 39.0 all-gather.5
  289.0 39.0 all-gather.3
where the time goes:
time: 347 us
  waiting for transfers between devices  313 us (90%)
  between operations  14.2 us (4%)
  local copies, waits for them, and re-layouts  12.3 us (4%)
  other arithmetic  7.5 us (2%)
    reduce_scatter x3, waiting for transfers between devices, step(): lax.psum_scatter(t[0], 'dp', scatter_dimension=1, tiled=True)  186 us
    all_gather x3, waiting for transfers between devices, step(): whole = [lax.all_gather(one[0], 'dp', axis=1, tiled=True) for one in new]  125 us
    unnamed x19, local copies, waits for them, and re-layouts  12.3 us
    convert_element_type x3, other arithmetic, adamw(): return ((w - 0.02 * step).astype(jnp.bfloat16), m, v)  7.5 us
  transfers between devices with their start and end apart: 6, of which 6 were waited for; matrix products, arithmetic and copies ran while one was open for 2% of the time, Pallas kernels for 0%

commit v1 on v0

v1 whole, which is shorter than its diff:
```python
import functools

import jax
import jax.numpy as jnp
from jax import lax
from jax.experimental import pallas as pl
from jax.experimental.pallas import tpu as pltpu
from jax.sharding import PartitionSpec as P

MESH = pl.DeviceIdType.MESH
CORES = 2
AHEAD = 2
TILE = 16


def adamw(w, m, v, g):
    m = 0.9 * m + 0.1 * g
    v = 0.95 * v + 0.05 * g * g
    step = m * lax.rsqrt(v + 1e-8) + 0.1 * w
    return (w - 0.02 * step).astype(jnp.bfloat16), m, v


def kernel(n, terms, weights, m_in, v_in, new, m_out, v_out, mine, theirs, partial, own_w, sems):
    (mine_sem, give_sem, take_sem, load_sem, sum_out, sum_in, ring_out, ring_in, fwd_out, fwd_in) = sems
    chips = n // CORES
    me = lax.axis_index("dp")
    chip, core = me // CORES, me % CORES
    way = 1 - CORES * core
    other = chip * CORES + (1 - core)

    def device_at(steps, which):
        return lax.rem(chip + way * steps + chips, chips) * CORES + which

    onward, behind = device_at(1, core), device_at(-1, core)
    layers = weights[0].shape[0]
    pieces = [(i, l) for i in range(len(terms)) for l in range(layers)]
    height = [ref.shape[2] for ref in mine]

    def rows(i, device):
        return pl.ds(pl.multiple_of(device * height[i], TILE), height[i])

    def fetch(s, p):
        i, l = pieces[p]
        return pltpu.make_async_copy(terms[i].at[0, l, rows(i, device_at(-1 - s, core))], mine[i].at[s, l], mine_sem.at[s, p])

    def give(s, p):
        i, l = pieces[p]
        return pltpu.make_async_remote_copy(
            src_ref=terms[i].at[0, l, rows(i, device_at(1 + s, 1 - core))],
            dst_ref=theirs[i].at[s, l],
            send_sem=give_sem.at[s, p],
            recv_sem=take_sem.at[s, p],
            device_id={"dp": other},
            device_id_type=MESH,
        )

    def send_sum(s, p):
        i, l = pieces[p]
        return pltpu.make_async_remote_copy(
            src_ref=mine[i].at[s, l],
            dst_ref=partial[i].at[s, l],
            send_sem=sum_out.at[s, p],
            recv_sem=sum_in.at[s, p],
            device_id={"dp": onward},
            device_id_type=MESH,
        )

    def send_new(s, p):
        i, l = pieces[p]
        block = new[i].at[l, rows(i, device_at(-s, core))]
        return pltpu.make_async_remote_copy(
            src_ref=block,
            dst_ref=block,
            send_sem=ring_out.at[s, p],
            recv_sem=ring_in.at[s, p],
            device_id={"dp": onward},
            device_id_type=MESH,
        )

    def forward(s, p):
        i, l = pieces[p]
        block = new[i].at[l, rows(i, device_at(-s, core))]
        return pltpu.make_async_remote_copy(
            src_ref=block,
            dst_ref=block,
            send_sem=fwd_out.at[s, p],
            recv_sem=fwd_in.at[s, p],
            device_id={"dp": other},
            device_id_type=MESH,
        )

    def loads():
        copies = []
        for i in range(len(terms)):
            copies.append(pltpu.make_async_copy(weights[i].at[:, rows(i, me)], own_w[i], load_sem.at[i]))
        return copies

    count = range(len(pieces))
    for s in range(min(AHEAD, chips)):
        for p in count:
            fetch(s, p).start()

    barrier = pltpu.get_barrier_semaphore()
    for device in (other, onward, behind):
        pl.semaphore_signal(barrier, inc=1, device_id={"dp": device}, device_id_type=MESH)
    pl.semaphore_wait(barrier, 3)

    for s in range(min(AHEAD, chips)):
        for p in count:
            give(s, p).start()
    for copy in loads():
        copy.start()

    def total(s, p, tile):
        i, l = pieces[p]
        at = pl.ds(pl.multiple_of(tile * TILE, TILE), TILE)
        g = mine[i][s, l, at].astype(jnp.float32) + theirs[i][s, l, at].astype(jnp.float32)
        if s > 0:
            g = g + partial[i][s - 1, l, at].astype(jnp.float32)
        return at, g.astype(jnp.bfloat16)

    for s in range(chips - 1):
        for p in count:
            if s + AHEAD < chips:
                fetch(s + AHEAD, p).start()
                give(s + AHEAD, p).start()
            i, l = pieces[p]
            fetch(s, p).wait()
            give(s, p).wait_recv()
            if s > 0:
                send_sum(s - 1, p).wait_recv()

            @pl.loop(0, height[i] // TILE)
            def _(tile):
                at, g = total(s, p, tile)
                mine[i][s, l, at] = g

            send_sum(s, p).start()

    for copy in loads():
        copy.wait()
    last = chips - 1
    for p in count:
        i, l = pieces[p]
        fetch(last, p).wait()
        give(last, p).wait_recv()
        send_sum(last - 1, p).wait_recv()
        mine_rows = pl.multiple_of(me * height[i], TILE)

        @pl.loop(0, height[i] // TILE)
        def _(tile):
            at, g = total(last, p, tile)
            w, m, v = adamw(own_w[i][l, at].astype(jnp.float32), m_in[i][l, at], v_in[i][l, at], g.astype(jnp.float32))
            new[i][l, pl.ds(pl.multiple_of(mine_rows + tile * TILE, TILE), TILE)] = w
            m_out[i][l, at] = m
            v_out[i][l, at] = v

        send_new(0, p).start()
        forward(0, p).start()
    for s in range(1, chips):
        for p in count:
            send_new(s - 1, p).wait_recv()
            if s < last:
                send_new(s, p).start()
            forward(s, p).start()
    for s in range(chips):
        for p in count:
            forward(s, p).wait_recv()
            forward(s, p).wait_send()
            give(s, p).wait_send()
            if s < last:
                send_sum(s, p).wait_send()
                send_new(s, p).wait_send()


def solution(mesh):
    n = mesh.shape["dp"]
    chips = n // CORES

    def step(*arrays):
        terms, weights, m, v = (arrays[i : i + 3] for i in (0, 3, 6, 9))
        blocks = [one.shape for one in m]
        layers = blocks[0][0]
        count = len(m) * layers
        dma = pltpu.SemaphoreType.DMA

        def body(*refs):
            parts = [refs[i : i + 3] for i in range(0, 33, 3)]
            kernel(n, *parts, refs[33:])

        per_step = [pltpu.VMEM((chips, *shape), jnp.bfloat16) for shape in blocks]
        hops = [pltpu.VMEM((chips - 1, *shape), jnp.bfloat16) for shape in blocks]
        scratch = [*per_step, *per_step, *hops, *(pltpu.VMEM(shape, jnp.bfloat16) for shape in blocks)]
        semaphores = [dma((chips, count))] * 3 + [dma((len(m),))] + [dma((chips - 1, count))] * 4 + [dma((chips, count))] * 2
        anywhere, vmem = pl.BlockSpec(memory_space=pl.ANY), pl.BlockSpec(memory_space=pltpu.VMEM)
        return pl.pallas_call(
            body,
            out_shape=[jax.ShapeDtypeStruct(w.shape, w.dtype) for w in weights] + [jax.ShapeDtypeStruct(s, jnp.float32) for s in blocks] * 2,
            in_specs=[anywhere] * 6 + [vmem] * 6,
            out_specs=[vmem] * 9,
            scratch_shapes=[*scratch, *semaphores],
            compiler_params=pltpu.CompilerParams(collective_id=0, has_side_effects=True),
        )(*arrays)

    all_of, cut = P(None, None, None), P(None, "dp", None)
    return jax.shard_map(
        step,
        mesh=mesh,
        in_specs=(P(("rep", "dp"), None, None, None),) * 3 + (all_of,) * 3 + (cut,) * 6,
        out_specs=(P("rep", None, None),) * 3 + (P("rep", "dp", None),) * 6,
        check_vma=False,
    )
```

time: 347 us -> 199 us (0.57)
  waiting for transfers between devices: 313 us -> 0 us
  Pallas kernels: 0 us -> 180 us
  between operations: 14.2 us -> 0.68 us
  other arithmetic: 7.5 us -> 0 us
  local copies, waits for them, and re-layouts: 12.3 us -> 18 us
    reduce_scatter x3 -> x0, waiting for transfers between devices: 186 us -> none  [step(): lax.psum_scatter(t[0], 'dp', scatter_dimension=1, tiled=True)]
    pallas_call x0 -> x1, Pallas kernels: none -> 180 us  [step(): pl.pallas_call(body, out_shape=[jax.ShapeDtypeStruct(w.shape, w.dtype) fo...]
    all_gather x3 -> x0, waiting for transfers between devices: 125 us -> none  [step(): whole = [lax.all_gather(one[0], 'dp', axis=1, tiled=True) for one in new]]
    convert_element_type x3 -> x0, other arithmetic: 7.5 us -> none  [adamw(): return ((w - 0.02 * step).astype(jnp.bfloat16), m, v)]
    unnamed x19 -> x25, local copies, waits for them, and re-layouts: 12.3 us -> 18 us
  transfers between devices with their start and end apart: 6 -> 0, of which waited for: 6 -> 0; matrix products, arithmetic and copies ran while one was open for 2% -> 0% of each run, Pallas kernels for 0% -> 0%
where the time goes in v1:
time: 199 us
  Pallas kernels  180 us (90%)
  local copies, waits for them, and re-layouts  18 us (9%)
    pallas_call x1, Pallas kernels, step(): pl.pallas_call(body, out_shape=[jax.ShapeDtypeStruct(w.shape, w.dtype) fo...  180 us
    unnamed x25, local copies, waits for them, and re-layouts  18 us

profile of v1, /device:TPU:21, one launch (start us, length us, event | category | flops | bytes accessed | tf_op | source)
XLA Modules:
  0.0 198.9 jit_solution(768515107961615618)
XLA Ops:
  0.6 180.2 %shard_map.187 = (bf16[2,768,1792]{2,1,0:T(8,128)(2,1)}, bf16[2,768,1792]{2,1,0:T(8,128)(2,1)}, bf16[2,1792,768]{2,1,0:T(8,128)(2,1)}, f32[2,48,1792]{2,1,0:T(8,...) custom-call(bf16[1,2,768,1792]{3,2,1,0:T(8,128)(2,1)} %refs_0_.1, ...), custom_call_target="tpu_custom_call" | custom-call | tf_op jit(solution)/shard_map/pallas_call | solution.py:196
  180.9 0.0 copy-start.1
  180.9 5.5 %copy.30 = bf16[2,768,1792]{2,1,0:T(8,128)(2,1)} copy(bf16[2,768,1792]{2,1,0:T(8,128)(2,1)} %get-tuple-element.18) | data formatting | bytes 11010048
  186.4 0.0 copy-done.1
  186.4 0.0 copy-start
  186.4 2.8 %copy.31 = bf16[2,768,1792]{2,1,0:T(8,128)(2,1)} copy(bf16[2,768,1792]{2,1,0:T(8,128)(2,1)S(1)} %copy-done.1) | data formatting | bytes 11010048
  189.2 1.7 copy-done
  191.0 0.0 copy-start.7
  191.0 0.0 copy-start.6
  191.0 0.0 copy-start.5
  191.0 0.0 copy-start.4
  191.0 0.0 copy-start.3
  191.0 2.8 %copy.32 = bf16[2,1792,768]{2,1,0:T(8,128)(2,1)} copy(bf16[2,1792,768]{2,1,0:T(8,128)(2,1)S(1)} %copy-done) | data formatting | bytes 11010048
  193.8 0.0 copy-done.7
  193.8 0.0 copy-start.2
  193.8 0.8 copy.33
  194.6 0.0 copy-done.6
  194.6 0.8 copy.34
  195.5 0.0 copy-done.5
  195.5 0.8 copy.35
  196.3 0.0 copy-done.4
  196.3 0.8 copy.36
  197.2 0.0 copy-done.3
  197.2 0.8 copy.37
  198.0 0.0 copy-done.2
  198.0 0.8 copy.38
Async XLA Ops:
  180.9 5.5 %copy-start.1 = (bf16[2,768,1792]{2,1,0:T(8,128)(2,1)S(1)}, bf16[2,768,1792]{2,1,0:T(8,128)(2,1)}, u32[]{:S(2)}) copy-start(bf16[2,768,1792]{2,1,0:T(8,128)(2,1)} %get-tuple-element.19) | copy-start | bytes 16515076
  186.4 4.5 %copy-start = (bf16[2,1792,768]{2,1,0:T(8,128)(2,1)S(1)}, bf16[2,1792,768]{2,1,0:T(8,128)(2,1)}, u32[]{:S(2)}) copy-start(bf16[2,1792,768]{2,1,0:T(8,128)(2,1)} %get-tuple-element.20) | copy-start | bytes 16515076
  191.0 2.8 %copy-start.7 = (f32[2,48,1792]{2,1,0:T(8,128)S(1)}, f32[2,48,1792]{2,1,0:T(8,128)}, u32[]{:S(2)}) copy-start(f32[2,48,1792]{2,1,0:T(8,128)} %get-tuple-element.21) | copy-start | bytes 2064388
  191.0 3.7 %copy-start.6 = (f32[2,48,1792]{2,1,0:T(8,128)S(1)}, f32[2,48,1792]{2,1,0:T(8,128)}, u32[]{:S(2)}) copy-start(f32[2,48,1792]{2,1,0:T(8,128)} %get-tuple-element.22) | copy-start | bytes 2064388
  191.0 4.5 %copy-start.5 = (f32[2,112,768]{2,1,0:T(8,128)S(1)}, f32[2,112,768]{2,1,0:T(8,128)}, u32[]{:S(2)}) copy-start(f32[2,112,768]{2,1,0:T(8,128)} %get-tuple-element.23) | copy-start | bytes 2064388
  191.0 5.4 %copy-start.4 = (f32[2,48,1792]{2,1,0:T(8,128)S(1)}, f32[2,48,1792]{2,1,0:T(8,128)}, u32[]{:S(2)}) copy-start(f32[2,48,1792]{2,1,0:T(8,128)} %get-tuple-element.24) | copy-start | bytes 2064388
  191.0 6.2 %copy-start.3 = (f32[2,48,1792]{2,1,0:T(8,128)S(1)}, f32[2,48,1792]{2,1,0:T(8,128)}, u32[]{:S(2)}) copy-start(f32[2,48,1792]{2,1,0:T(8,128)} %get-tuple-element.25) | copy-start | bytes 2064388
  193.8 4.3 %copy-start.2 = (f32[2,112,768]{2,1,0:T(8,128)S(1)}, f32[2,112,768]{2,1,0:T(8,128)}, u32[]{:S(2)}) copy-start(f32[2,112,768]{2,1,0:T(8,128)} %get-tuple-element.26) | copy-start | bytes 2064388

commit v2 on v1

--- a/solution.py
+++ b/solution.py
@@ -11,6 +11,8 @@
 CORES = 2
 AHEAD = 2
 TILE = 16
+SCRATCH_BYTES = 43 << 20
+WRITE_BYTES = 1 << 20
 
 
 def adamw(w, m, v, g):
@@ -20,7 +22,16 @@
     return (w - 0.02 * step).astype(jnp.bfloat16), m, v
 
 
-def kernel(n, terms, weights, m_in, v_in, new, m_out, v_out, mine, theirs, partial, own_w, sems):
+def write_out(count, *refs):
+    sources, places, sem = refs[:count], refs[count : 2 * count], refs[-1]
+    copies = [pltpu.make_async_copy(a, b, sem.at[k]) for k, (a, b) in enumerate(zip(sources, places, strict=True))]
+    for copy in copies:
+        copy.start()
+    for copy in copies:
+        copy.wait()
+
+
+def kernel(n, terms, weights, m_from, v_from, new, m_out, v_out, mine, theirs, partial, own_w, m_in, v_in, sems):
     (mine_sem, give_sem, take_sem, load_sem, sum_out, sum_in, ring_out, ring_in, fwd_out, fwd_in) = sems
     chips = n // CORES
     me = lax.axis_index("dp")
@@ -92,7 +103,9 @@
     def loads():
         copies = []
         for i in range(len(terms)):
-            copies.append(pltpu.make_async_copy(weights[i].at[:, rows(i, me)], own_w[i], load_sem.at[i]))
+            copies.append(pltpu.make_async_copy(weights[i].at[:, rows(i, me)], own_w[i], load_sem.at[0, i]))
+            copies.append(pltpu.make_async_copy(m_from[i], m_in[i], load_sem.at[1, i]))
+            copies.append(pltpu.make_async_copy(v_from[i], v_in[i], load_sem.at[2, i]))
         return copies
 
     count = range(len(pieces))
@@ -185,22 +198,32 @@
         dma = pltpu.SemaphoreType.DMA
 
         def body(*refs):
-            parts = [refs[i : i + 3] for i in range(0, 33, 3)]
-            kernel(n, *parts, refs[33:])
+            parts = [refs[i : i + 3] for i in range(0, 39, 3)]
+            kernel(n, *parts, refs[39:])
 
         per_step = [pltpu.VMEM((chips, *shape), jnp.bfloat16) for shape in blocks]
         hops = [pltpu.VMEM((chips - 1, *shape), jnp.bfloat16) for shape in blocks]
-        scratch = [*per_step, *per_step, *hops, *(pltpu.VMEM(shape, jnp.bfloat16) for shape in blocks)]
-        semaphores = [dma((chips, count))] * 3 + [dma((len(m),))] + [dma((chips - 1, count))] * 4 + [dma((chips, count))] * 2
-        anywhere, vmem = pl.BlockSpec(memory_space=pl.ANY), pl.BlockSpec(memory_space=pltpu.VMEM)
+        moments = [pltpu.VMEM(shape, jnp.float32) for shape in blocks]
+        scratch = [*per_step, *per_step, *hops, *(pltpu.VMEM(shape, jnp.bfloat16) for shape in blocks), *moments, *moments]
+        semaphores = [dma((chips, count))] * 3 + [dma((3, len(m)))] + [dma((chips - 1, count))] * 4 + [dma((chips, count))] * 2
+        hbm, vmem = pl.BlockSpec(memory_space=pltpu.HBM), pl.BlockSpec(memory_space=pltpu.VMEM)
+        shapes = [jax.ShapeDtypeStruct(w.shape, w.dtype) for w in weights] + [jax.ShapeDtypeStruct(s, jnp.float32) for s in blocks] * 2
+        inside = pl.pallas_call(
+            body,
+            out_shape=[pltpu.VMEM(one.shape, one.dtype) for one in shapes],
+            in_specs=[hbm] * len(arrays),
+            out_specs=[vmem] * len(shapes),
+            scratch_shapes=[*scratch, *semaphores],
+            compiler_params=pltpu.CompilerParams(collective_id=0, has_side_effects=True, vmem_limit_bytes=SCRATCH_BYTES),
+        )(*arrays)
         return pl.pallas_call(
-            body,
-            out_shape=[jax.ShapeDtypeStruct(w.shape, w.dtype) for w in weights] + [jax.ShapeDtypeStruct(s, jnp.float32) for s in blocks] * 2,
-            in_specs=[anywhere] * 6 + [vmem] * 6,
-            out_specs=[vmem] * 9,
-            scratch_shapes=[*scratch, *semaphores],
-            compiler_params=pltpu.CompilerParams(collective_id=0, has_side_effects=True),
-        )(*arrays)
+            functools.partial(write_out, len(shapes)),
+            out_shape=shapes,
+            in_specs=[vmem] * len(shapes),
+            out_specs=[hbm] * len(shapes),
+            scratch_shapes=[dma((len(shapes),))],
+            compiler_params=pltpu.CompilerParams(vmem_limit_bytes=WRITE_BYTES),
+        )(*inside)
 
     all_of, cut = P(None, None, None), P(None, "dp", None)
     return jax.shard_map(

time: 199 us -> 179 us (0.90)
  local copies, waits for them, and re-layouts: 18 us -> 0 us
  Pallas kernels: 180 us -> 178 us
    unnamed x25 -> x0, local copies, waits for them, and re-layouts: 18 us -> none
    pallas_call x1 -> x2, Pallas kernels: 180 us -> 178 us  [the longest x1 171 us: step(): pl.pallas_call(body, out_shape=[pltpu.VMEM(one.shape, one.dtype) for one...]
where the time goes in v2:
time: 179 us
  Pallas kernels  178 us (99%)
    pallas_call x1, Pallas kernels, step(): pl.pallas_call(body, out_shape=[pltpu.VMEM(one.shape, one.dtype) for one...  171 us
    pallas_call x1, Pallas kernels, step(): pl.pallas_call(functools.partial(write_out, len(shapes)), out_shape=shape...  7.09 us

profile of v2, /device:TPU:21, one launch (start us, length us, event | category | flops | bytes accessed | tf_op | source)
XLA Modules:
  0.0 179.1 jit_solution(8200030809961273445)
XLA Ops:
  0.6 171.3 %shard_map.187 = (bf16[2,768,1792]{2,1,0:T(8,128)(2,1)S(1)}, bf16[2,768,1792]{2,1,0:T(8,128)(2,1)S(1)}, bf16[2,1792,768]{2,1,0:T(8,128)(2,1)S(1)}, f32[2,48,1792...) custom-call(bf16[1,2,768,1792]{3,2,1,0:T(8,128)(2,1)} %refs_0_.1, ...), custom_call_target="tpu_custom_call" | custom-call | tf_op jit(solution)/shard_map/pallas_call | solution.py:211
  172.0 7.1 %shard_map.188 = (bf16[2,768,1792]{2,1,0:T(8,128)(2,1)}, bf16[2,768,1792]{2,1,0:T(8,128)(2,1)}, bf16[2,1792,768]{2,1,0:T(8,128)(2,1)}, f32[2,48,1792]{2,1,0:T(8,...) custom-call(bf16[2,768,1792]{2,1,0:T(8,128)(2,1)S(1)} %get-tuple-ele, ...), custom_call_target="tpu_custom_call" | custom-call | tf_op jit(solution)/shard_map/pallas_call | solution.py:219

commit v3 on v0

v3 whole, which is shorter than its diff:
```python
import functools

import jax
import jax.numpy as jnp
from jax import lax
from jax.experimental import pallas as pl
from jax.experimental.pallas import tpu as pltpu
from jax.sharding import PartitionSpec as P

MESH = pl.DeviceIdType.MESH
CORES = 2
AHEAD = 2
TILE = 16
SCRATCH_BYTES = 43 << 20
WRITE_BYTES = 1 << 20


def adamw(w, m, v, g):
    m = 0.9 * m + 0.1 * g
    v = 0.95 * v + 0.05 * g * g
    step = m * lax.rsqrt(v + 1e-8) + 0.1 * w
    return (w - 0.02 * step).astype(jnp.bfloat16), m, v


def write_out(count, *refs):
    sources, places, sem = refs[:count], refs[count : 2 * count], refs[-1]
    copies = [pltpu.make_async_copy(a, b, sem.at[k]) for k, (a, b) in enumerate(zip(sources, places, strict=True))]
    for copy in copies:
        copy.start()
    for copy in copies:
        copy.wait()


def cut(blocks, first, last):
    coarse = [(i, (0, shape[0]), (0, shape[1])) for i, shape in enumerate(blocks)]
    single = [(i, (l, l + 1), (0, shape[1])) for i, shape in enumerate(blocks) for l in range(shape[0])]

    def split(piece, parts):
        i, layers, (low, high) = piece
        tiles, at, out = (high - low) // TILE, low, []
        for k in range(parts):
            size = (tiles // (parts - k)) * TILE
            tiles -= size // TILE
            out.append((i, layers, (at, at + size)))
            at += size
        return out

    fine_first = [*split(single[0], first), *single[1:]]
    fine_last = [*single[:-1], *split(single[-1], last)]
    return coarse, fine_first, fine_last


def kernel(n, cuts, terms, weights, m_from, v_from, new, m_out, v_out, mine, theirs, partial, own_w, m_in, v_in, stage, sems):
    (mine_sem, stage_sem, give_sem, take_sem, load_sem, sum_out, sum_in, ring_out, ring_in, fwd_out, fwd_in) = sems
    coarse, fine_first, fine_last = cuts
    chips = n // CORES
    last = chips - 1
    me = lax.axis_index("dp")
    chip, core = me // CORES, me % CORES
    way = 1 - CORES * core
    other = chip * CORES + (1 - core)

    def device_at(steps, which):
        return lax.rem(chip + way * steps + chips, chips) * CORES + which

    onward, behind = device_at(1, core), device_at(-1, core)
    height = [ref.shape[2] for ref in mine]

    def remote(source, place, send_sem, recv_sem, device):
        return pltpu.make_async_remote_copy(
            src_ref=source, dst_ref=place, send_sem=send_sem, recv_sem=recv_sem, device_id={"dp": device}, device_id_type=MESH
        )

    def span(piece):
        _, (l0, l1), (r0, r1) = piece
        return pl.ds(l0, l1 - l0), pl.ds(r0, r1 - r0)

    def rows(piece, device):
        i, _, (r0, r1) = piece
        return pl.ds(pl.multiple_of(device * height[i] + r0, TILE), r1 - r0)

    def cut_of_sum(s):
        return fine_first if s == 0 else coarse

    def cut_of_new(s):
        return fine_last if s >= last - 1 else coarse

    def fetch(s, p):
        piece = cut_of_sum(s)[p]
        layers, within = span(piece)
        source = terms[piece[0]].at[0, layers, rows(piece, device_at(-1 - s, core))]
        return pltpu.make_async_copy(source, mine[piece[0]].at[s, layers, within], mine_sem.at[s, p])

    def set_stage(p):
        piece = cut_of_sum(0)[p]
        layers, within = span(piece)
        source = terms[piece[0]].at[0, layers, rows(piece, device_at(1, 1 - core))]
        return pltpu.make_async_copy(source, stage[piece[0]].at[layers, within], stage_sem.at[p])

    def give(s, p):
        piece = cut_of_sum(s)[p]
        layers, within = span(piece)
        if s == 0:
            source = stage[piece[0]].at[layers, within]
        else:
            source = terms[piece[0]].at[0, layers, rows(piece, device_at(1 + s, 1 - core))]
        return remote(source, theirs[piece[0]].at[s, layers, within], give_sem.at[s, p], take_sem.at[s, p], other)

    def send_sum(s, p):
        piece = cut_of_sum(s)[p]
        layers, within = span(piece)
        i = piece[0]
        return remote(mine[i].at[s, layers, within], partial[i].at[s, layers, within], sum_out.at[s, p], sum_in.at[s, p], onward)

    def new_block(s, piece):
        return new[piece[0]].at[span(piece)[0], rows(piece, device_at(-s, core))]

    def send_new(s, p):
        block = new_block(s, cut_of_new(s)[p])
        return remote(block, block, ring_out.at[s, p], ring_in.at[s, p], onward)

    def forward(s, p):
        block = new_block(s, cut_of_new(max(s - 1, 0))[p])
        return remote(block, block, fwd_out.at[s, p], fwd_in.at[s, p], other)

    def load(i):
        return [
            pltpu.make_async_copy(weights[i].at[:, pl.ds(pl.multiple_of(me * height[i], TILE), height[i])], own_w[i], load_sem.at[0, i]),
            pltpu.make_async_copy(m_from[i], m_in[i], load_sem.at[1, i]),
            pltpu.make_async_copy(v_from[i], v_in[i], load_sem.at[2, i]),
        ]

    def every(s):
        return range(len(cut_of_sum(s)))

    barrier = pltpu.get_barrier_semaphore()
    for device in (other, onward, behind):
        pl.semaphore_signal(barrier, inc=1, device_id={"dp": device}, device_id_type=MESH)
    for p in every(0):
        set_stage(p).start()
        fetch(0, p).start()
    set_stage(0).wait()
    pl.semaphore_wait(barrier, 3)
    for p in every(0):
        if p:
            set_stage(p).wait()
        give(0, p).start()
    for s in range(1, AHEAD):
        for p in every(s):
            fetch(s, p).start()
            give(s, p).start()

    def over_tiles(piece, do):
        i, (l0, l1), (r0, r1) = piece
        for l in range(l0, l1):

            @pl.loop(r0 // TILE, r1 // TILE)
            def _(tile):
                do(i, l, tile, pl.ds(pl.multiple_of(tile * TILE, TILE), TILE))

    def total(s, i, l, at):
        g = mine[i][s, l, at].astype(jnp.float32) + theirs[i][s, l, at].astype(jnp.float32)
        if s > 0:
            g = g + partial[i][s - 1, l, at].astype(jnp.float32)
        return g.astype(jnp.bfloat16)

    def wait_parts(s, p):
        for q, piece in enumerate(cut_of_sum(s - 1)):
            if piece[0] == cut_of_sum(s)[p][0]:
                send_sum(s - 1, q).wait_recv()

    for s in range(chips - 1):
        for p in every(s):
            fetch(s, p).wait()
            give(s, p).wait_recv()
            if s > 0:
                wait_parts(s, p)

            def add(i, l, tile, at):
                mine[i][s, l, at] = total(s, i, l, at)

            over_tiles(cut_of_sum(s)[p], add)
            send_sum(s, p).start()
        if s + AHEAD < chips:
            for p in every(s + AHEAD):
                fetch(s + AHEAD, p).start()
                give(s + AHEAD, p).start()
        if s == 0:
            for i in range(len(weights)):
                for copy in load(i):
                    copy.start()

    for p, piece in enumerate(coarse):
        i = piece[0]
        for copy in load(i):
            copy.wait()
        fetch(last, p).wait()
        give(last, p).wait_recv()
        wait_parts(last, p)
        start = pl.multiple_of(me * height[i], TILE)

        def take_step(i, l, tile, at):
            g = total(last, i, l, at).astype(jnp.float32)
            w, m, v = adamw(own_w[i][l, at].astype(jnp.float32), m_in[i][l, at], v_in[i][l, at], g)
            new[i][l, pl.ds(pl.multiple_of(start + tile * TILE, TILE), TILE)] = w
            m_out[i][l, at] = m
            v_out[i][l, at] = v

        over_tiles(piece, take_step)
        send_new(0, p).start()
        forward(0, p).start()
    for s in range(1, chips):
        came = cut_of_new(s - 1)
        if s < last and cut_of_new(s) is not came:
            for p, piece in enumerate(came):
                send_new(s - 1, p).wait_recv()
                for q, finer in enumerate(cut_of_new(s)):
                    if finer[0] == piece[0]:
                        send_new(s, q).start()
                forward(s, p).start()
        else:
            for p in range(len(came)):
                send_new(s - 1, p).wait_recv()
                if s < last:
                    send_new(s, p).start()
                forward(s, p).start()
    for s in range(chips):
        for p in every(s):
            give(s, p).wait_send()
            if s < last:
                send_sum(s, p).wait_send()
        for p in range(len(cut_of_new(s))):
            if s < last:
                send_new(s, p).wait_send()
        for p in range(len(cut_of_new(max(s - 1, 0)))):
            forward(s, p).wait_send()
            forward(s, p).wait_recv()


def solution(mesh):
    n = mesh.shape["dp"]
    chips = n // CORES

    def step(*arrays):
        terms, weights, m, v = (arrays[i : i + 3] for i in (0, 3, 6, 9))
        blocks = [one.shape for one in m]
        cuts = cut(blocks, 3, 3)
        count = max(len(one) for one in cuts)
        dma = pltpu.SemaphoreType.DMA

        def body(*refs):
            parts = [refs[i : i + 3] for i in range(0, 42, 3)]
            kernel(n, cuts, *parts, refs[42:])

        per_step = [pltpu.VMEM((chips, *shape), jnp.bfloat16) for shape in blocks]
        hops = [pltpu.VMEM((chips - 1, *shape), jnp.bfloat16) for shape in blocks]
        block = [pltpu.VMEM(shape, jnp.bfloat16) for shape in blocks]
        moments = [pltpu.VMEM(shape, jnp.float32) for shape in blocks]
        scratch = [*per_step, *per_step, *hops, *block, *moments, *moments, *block]
        semaphores = [
            dma((chips, count)),
            dma((count,)),
            *[dma((chips, count))] * 2,
            dma((3, len(m))),
            *[dma((chips - 1, count))] * 4,
            *[dma((chips, count))] * 2,
        ]
        hbm, vmem = pl.BlockSpec(memory_space=pltpu.HBM), pl.BlockSpec(memory_space=pltpu.VMEM)
        shapes = [jax.ShapeDtypeStruct(w.shape, w.dtype) for w in weights] + [jax.ShapeDtypeStruct(s, jnp.float32) for s in blocks] * 2
        inside = pl.pallas_call(
            body,
            out_shape=[pltpu.VMEM(one.shape, one.dtype) for one in shapes],
            in_specs=[hbm] * len(arrays),
            out_specs=[vmem] * len(shapes),
            scratch_shapes=[*scratch, *semaphores],
            compiler_params=pltpu.CompilerParams(collective_id=0, has_side_effects=True, vmem_limit_bytes=SCRATCH_BYTES),
        )(*arrays)
        return pl.pallas_call(
            functools.partial(write_out, len(shapes)),
            out_shape=shapes,
            in_specs=[vmem] * len(shapes),
            out_specs=[hbm] * len(shapes),
            scratch_shapes=[dma((len(shapes),))],
            compiler_params=pltpu.CompilerParams(vmem_limit_bytes=WRITE_BYTES),
        )(*inside)

    all_of, shared = P(None, None, None), P(None, "dp", None)
    return jax.shard_map(
        step,
        mesh=mesh,
        in_specs=(P(("rep", "dp"), None, None, None),) * 3 + (all_of,) * 3 + (shared,) * 6,
        out_specs=(P("rep", None, None),) * 3 + (P("rep", "dp", None),) * 6,
        check_vma=False,
    )
```

time: 347 us -> 180 us (0.52)
  waiting for transfers between devices: 313 us -> 0 us
  Pallas kernels: 0 us -> 180 us
  between operations: 14.2 us -> 0.65 us
  local copies, waits for them, and re-layouts: 12.3 us -> 0 us
  other arithmetic: 7.5 us -> 0 us
    reduce_scatter x3 -> x0, waiting for transfers between devices: 186 us -> none  [step(): lax.psum_scatter(t[0], 'dp', scatter_dimension=1, tiled=True)]
    pallas_call x0 -> x2, Pallas kernels: none -> 180 us  [the longest x1 173 us: step(): pl.pallas_call(body, out_shape=[pltpu.VMEM(one.shape, one.dtype) for one...]
    all_gather x3 -> x0, waiting for transfers between devices: 125 us -> none  [step(): whole = [lax.all_gather(one[0], 'dp', axis=1, tiled=True) for one in new]]
    unnamed x19 -> x0, local copies, waits for them, and re-layouts: 12.3 us -> none
    convert_element_type x3 -> x0, other arithmetic: 7.5 us -> none  [adamw(): return ((w - 0.02 * step).astype(jnp.bfloat16), m, v)]
  transfers between devices with their start and end apart: 6 -> 0, of which waited for: 6 -> 0; matrix products, arithmetic and copies ran while one was open for 2% -> 0% of each run, Pallas kernels for 0% -> 0%
where the time goes in v3:
time: 180 us
  Pallas kernels  180 us (100%)
    pallas_call x1, Pallas kernels, step(): pl.pallas_call(body, out_shape=[pltpu.VMEM(one.shape, one.dtype) for one...  173 us
    pallas_call x1, Pallas kernels, step(): pl.pallas_call(functools.partial(write_out, len(shapes)), out_shape=shape...  7.09 us

profile of v3, /device:TPU:21, one launch (start us, length us, event | category | flops | bytes accessed | tf_op | source)
XLA Modules:
  0.0 180.4 jit_solution(14170609535500008760)
XLA Ops:
  0.6 172.6 %shard_map.187 = (bf16[2,768,1792]{2,1,0:T(8,128)(2,1)S(1)}, bf16[2,768,1792]{2,1,0:T(8,128)(2,1)S(1)}, bf16[2,1792,768]{2,1,0:T(8,128)(2,1)S(1)}, f32[2,48,1792...) custom-call(bf16[1,2,768,1792]{3,2,1,0:T(8,128)(2,1)} %refs_0_.1, ...), custom_call_target="tpu_custom_call" | custom-call | tf_op jit(solution)/shard_map/pallas_call | solution.py:270
  173.3 7.1 %shard_map.188 = (bf16[2,768,1792]{2,1,0:T(8,128)(2,1)}, bf16[2,768,1792]{2,1,0:T(8,128)(2,1)}, bf16[2,1792,768]{2,1,0:T(8,128)(2,1)}, f32[2,48,1792]{2,1,0:T(8,...) custom-call(bf16[2,768,1792]{2,1,0:T(8,128)(2,1)S(1)} %get-tuple-ele, ...), custom_call_target="tpu_custom_call" | custom-call | tf_op jit(solution)/shard_map/pallas_call | solution.py:278

commit v4 on v3

--- a/solution.py
+++ b/solution.py
@@ -10,6 +10,10 @@
 MESH = pl.DeviceIdType.MESH
 CORES = 2
 AHEAD = 2
+FIRST = 1
+LAST = 1
+COARSE = True
+STAGE = False
 TILE = 16
 SCRATCH_BYTES = 43 << 20
 WRITE_BYTES = 1 << 20
@@ -47,7 +51,12 @@
 
     fine_first = [*split(single[0], first), *single[1:]]
     fine_last = [*single[:-1], *split(single[-1], last)]
-    return coarse, fine_first, fine_last
+    return coarse if COARSE else single, fine_first, fine_last
+
+
+def inside(small, large):
+    (i, (l0, l1), (r0, r1)), (j, (k0, k1), (q0, q1)) = small, large
+    return i == j and k0 <= l0 and l1 <= k1 and q0 <= r0 and r1 <= q1
 
 
 def kernel(n, cuts, terms, weights, m_from, v_from, new, m_out, v_out, mine, theirs, partial, own_w, m_in, v_in, stage, sems):
@@ -100,28 +109,30 @@
     def give(s, p):
         piece = cut_of_sum(s)[p]
         layers, within = span(piece)
-        if s == 0:
+        if s == 0 and STAGE:
             source = stage[piece[0]].at[layers, within]
         else:
             source = terms[piece[0]].at[0, layers, rows(piece, device_at(1 + s, 1 - core))]
-        return remote(source, theirs[piece[0]].at[s, layers, within], give_sem.at[s, p], take_sem.at[s, p], other)
+        return remote(source, theirs[piece[0]].at[s, layers, within], give_sem.at[piece[0]], take_sem.at[s, p], other)
 
     def send_sum(s, p):
         piece = cut_of_sum(s)[p]
         layers, within = span(piece)
         i = piece[0]
-        return remote(mine[i].at[s, layers, within], partial[i].at[s, layers, within], sum_out.at[s, p], sum_in.at[s, p], onward)
+        return remote(mine[i].at[s, layers, within], partial[i].at[s, layers, within], sum_out.at[i], sum_in.at[s, p], onward)
 
     def new_block(s, piece):
         return new[piece[0]].at[span(piece)[0], rows(piece, device_at(-s, core))]
 
     def send_new(s, p):
-        block = new_block(s, cut_of_new(s)[p])
-        return remote(block, block, ring_out.at[s, p], ring_in.at[s, p], onward)
+        piece = cut_of_new(s)[p]
+        block = new_block(s, piece)
+        return remote(block, block, ring_out.at[piece[0]], ring_in.at[s, p], onward)
 
     def forward(s, p):
-        block = new_block(s, cut_of_new(max(s - 1, 0))[p])
-        return remote(block, block, fwd_out.at[s, p], fwd_in.at[s, p], other)
+        piece = cut_of_new(max(s - 1, 0))[p]
+        block = new_block(s, piece)
+        return remote(block, block, fwd_out.at[piece[0]], fwd_in.at[piece[0]], other)
 
     def load(i):
         return [
@@ -137,12 +148,14 @@
     for device in (other, onward, behind):
         pl.semaphore_signal(barrier, inc=1, device_id={"dp": device}, device_id_type=MESH)
     for p in every(0):
-        set_stage(p).start()
+        if STAGE:
+            set_stage(p).start()
         fetch(0, p).start()
-    set_stage(0).wait()
+    if STAGE:
+        set_stage(0).wait()
     pl.semaphore_wait(barrier, 3)
     for p in every(0):
-        if p:
+        if p and STAGE:
             set_stage(p).wait()
         give(0, p).start()
     for s in range(1, AHEAD):
@@ -166,7 +179,7 @@
 
     def wait_parts(s, p):
         for q, piece in enumerate(cut_of_sum(s - 1)):
-            if piece[0] == cut_of_sum(s)[p][0]:
+            if inside(piece, cut_of_sum(s)[p]):
                 send_sum(s - 1, q).wait_recv()
 
     for s in range(chips - 1):
@@ -192,8 +205,9 @@
 
     for p, piece in enumerate(coarse):
         i = piece[0]
-        for copy in load(i):
-            copy.wait()
+        if p == 0 or coarse[p - 1][0] != i:
+            for copy in load(i):
+                copy.wait()
         fetch(last, p).wait()
         give(last, p).wait_recv()
         wait_parts(last, p)
@@ -215,7 +229,7 @@
             for p, piece in enumerate(came):
                 send_new(s - 1, p).wait_recv()
                 for q, finer in enumerate(cut_of_new(s)):
-                    if finer[0] == piece[0]:
+                    if inside(finer, piece):
                         send_new(s, q).start()
                 forward(s, p).start()
         else:
@@ -224,17 +238,14 @@
                 if s < last:
                     send_new(s, p).start()
                 forward(s, p).start()
-    for s in range(chips):
-        for p in every(s):
-            give(s, p).wait_send()
-            if s < last:
-                send_sum(s, p).wait_send()
-        for p in range(len(cut_of_new(s))):
-            if s < last:
-                send_new(s, p).wait_send()
-        for p in range(len(cut_of_new(max(s - 1, 0)))):
-            forward(s, p).wait_send()
-            forward(s, p).wait_recv()
+    for i in range(len(terms)):
+        some = new[i].at[:, pl.ds(0, last * height[i])]
+        remote(theirs[i], theirs[i], give_sem.at[i], fwd_in.at[i], other).wait_send()
+        remote(partial[i], partial[i], sum_out.at[i], fwd_in.at[i], onward).wait_send()
+        remote(some, some, ring_out.at[i], fwd_in.at[i], onward).wait_send()
+        whole = remote(theirs[i], theirs[i], fwd_out.at[i], fwd_in.at[i], other)
+        whole.wait_send()
+        whole.wait_recv()
 
 
 def solution(mesh):
@@ -244,7 +255,7 @@
     def step(*arrays):
         terms, weights, m, v = (arrays[i : i + 3] for i in (0, 3, 6, 9))
         blocks = [one.shape for one in m]
-        cuts = cut(blocks, 3, 3)
+        cuts = cut(blocks, FIRST, LAST)
         count = max(len(one) for one in cuts)
         dma = pltpu.SemaphoreType.DMA
 
@@ -257,16 +268,11 @@
         block = [pltpu.VMEM(shape, jnp.bfloat16) for shape in blocks]
         moments = [pltpu.VMEM(shape, jnp.float32) for shape in blocks]
         scratch = [*per_step, *per_step, *hops, *block, *moments, *moments, *block]
-        semaphores = [
-            dma((chips, count)),
-            dma((count,)),
-            *[dma((chips, count))] * 2,
-            dma((3, len(m))),
-            *[dma((chips - 1, count))] * 4,
-            *[dma((chips, count))] * 2,
-        ]
+        each, hop = dma((chips, count)), dma((chips - 1, count))
+        one = dma((len(m),))
+        semaphores = [each, dma((count,)), one, each, dma((3, len(m))), one, hop, one, hop, one, one]
         hbm, vmem = pl.BlockSpec(memory_space=pltpu.HBM), pl.BlockSpec(memory_space=pltpu.VMEM)
-        shapes = [jax.ShapeDtypeStruct(w.shape, w.dtype) for w in weights] + [jax.ShapeDtypeStruct(s, jnp.float32) for s in blocks] * 2
+        shapes = [jax.ShapeDtypeStruct(w.shape, w.dtype) for w in weights] + [jax.ShapeDtypeStruct(b, jnp.float32) for b in blocks] * 2
         inside = pl.pallas_call(
             body,
             out_shape=[pltpu.VMEM(one.shape, one.dtype) for one in shapes],

time: 180 us -> 177 us (0.983)
  Pallas kernels: 180 us -> 177 us
    pallas_call x1, Pallas kernels: 173 us -> 169 us  [step(): pl.pallas_call(body, out_shape=[pltpu.VMEM(one.shape, one.dtype) for one...]
where the time goes in v4:
time: 177 us
  Pallas kernels  177 us (100%)
    pallas_call x1, Pallas kernels, step(): pl.pallas_call(body, out_shape=[pltpu.VMEM(one.shape, one.dtype) for one...  169 us
    pallas_call x1, Pallas kernels, step(): pl.pallas_call(functools.partial(write_out, len(shapes)), out_shape=shape...  7.09 us

profile of v4, /device:TPU:21, one launch (start us, length us, event | category | flops | bytes accessed | tf_op | source)
XLA Modules:
  0.0 177.2 jit_solution(6753077257453390928)
XLA Ops:
  0.6 169.4 %shard_map.187 = (bf16[2,768,1792]{2,1,0:T(8,128)(2,1)S(1)}, bf16[2,768,1792]{2,1,0:T(8,128)(2,1)S(1)}, bf16[2,1792,768]{2,1,0:T(8,128)(2,1)S(1)}, f32[2,48,1792...) custom-call(bf16[1,2,768,1792]{3,2,1,0:T(8,128)(2,1)} %refs_0_.1, ...), custom_call_target="tpu_custom_call" | custom-call | tf_op jit(solution)/shard_map/pallas_call | solution.py:276
  170.1 7.1 %shard_map.188 = (bf16[2,768,1792]{2,1,0:T(8,128)(2,1)}, bf16[2,768,1792]{2,1,0:T(8,128)(2,1)}, bf16[2,1792,768]{2,1,0:T(8,128)(2,1)}, f32[2,48,1792]{2,1,0:T(8,...) custom-call(bf16[2,768,1792]{2,1,0:T(8,128)(2,1)S(1)} %get-tuple-ele, ...), custom_call_target="tpu_custom_call" | custom-call | tf_op jit(solution)/shard_map/pallas_call | solution.py:284

commit v5 on v0

v5 whole, which is shorter than its diff:
```python
import functools

import jax
import jax.numpy as jnp
from jax import lax
from jax.experimental import pallas as pl
from jax.experimental.pallas import tpu as pltpu
from jax.sharding import PartitionSpec as P

MESH = pl.DeviceIdType.MESH
CORES = 2
AHEAD = 2
FIRST = (1,)
LAST = (1, 2)
TILE = 16
SCRATCH_BYTES = 43 << 20
WRITE_BYTES = 1 << 20


def adamw(w, m, v, g):
    m = 0.9 * m + 0.1 * g
    v = 0.95 * v + 0.05 * g * g
    step = m * lax.rsqrt(v + 1e-8) + 0.1 * w
    return (w - 0.02 * step).astype(jnp.bfloat16), m, v


def write_out(count, *refs):
    sources, places, sem = refs[:count], refs[count : 2 * count], refs[-1]
    copies = [pltpu.make_async_copy(a, b, sem.at[k]) for k, (a, b) in enumerate(zip(sources, places, strict=True))]
    for copy in copies:
        copy.start()
    for copy in copies:
        copy.wait()


def cut(shape, sizes, backwards):
    layers, height = shape[:2]
    ends, at = [], 0
    for size in sizes:
        ends.append((at, at + size * TILE))
        at += size * TILE
    ends.append((at, height))
    if backwards:
        ends = [(height - high, height - low) for low, high in reversed(ends)]
        return [((0, layers - 1), (0, height)), *[((layers - 1, layers), one) for one in ends]]
    return [*[((0, 1), one) for one in ends], ((1, layers), (0, height))]


def kernel(n, terms, weights, m_from, v_from, new, m_out, v_out, mine, theirs, partial, own_w, m_in, v_in, sems):
    mine_sem, take_sem, first_sem, hop_sem, end_sem, load_sem, chip_out, ring_out, fwd_in = sems
    chips = n // CORES
    last = chips - 1
    me = lax.axis_index("dp")
    chip, core = me // CORES, me % CORES
    way = 1 - CORES * core
    other = chip * CORES + (1 - core)
    shapes = [ref.shape[1:] for ref in mine]
    height = [shape[1] for shape in shapes]
    every = range(len(terms))
    whole = [[((0, shape[0]), (0, shape[1]))] for shape in shapes]
    first, final = [*whole], [*whole]
    first[0] = cut(shapes[0], FIRST, False)
    final[-1] = cut(shapes[-1], LAST, True)

    def device_at(steps, which):
        return lax.rem(chip + way * steps + chips, chips) * CORES + which

    onward = device_at(1, core)

    def remote(source, place, send_sem, recv_sem, device):
        return pltpu.make_async_remote_copy(
            src_ref=source, dst_ref=place, send_sem=send_sem, recv_sem=recv_sem, device_id={"dp": device}, device_id_type=MESH
        )

    def rows(i, device, part=None):
        low, high = part or (0, height[i])
        return pl.ds(pl.multiple_of(device * height[i] + low, TILE), high - low)

    def span(low, high):
        return pl.ds(low, high - low)

    def fetch(s, i):
        source = terms[i].at[0, :, rows(i, device_at(-1 - s, core))]
        return pltpu.make_async_copy(source, mine[i].at[s], mine_sem.at[s % AHEAD, i])

    def parts_of_sum(s, i):
        return first[i] if s == 0 else whole[i]

    def parts_of_new(s, i):
        return final[i] if s == last - 1 else whole[i]

    def give(s, i, k):
        layers, part = parts_of_sum(s, i)[k]
        sem = first_sem.at[k] if len(parts_of_sum(s, i)) > 1 else take_sem.at[s % (2 * AHEAD), i]
        source = terms[i].at[0, span(*layers), rows(i, device_at(1 + s, 1 - core), part)]
        return remote(source, theirs[i].at[s, span(*layers), span(*part)], chip_out.at[i], sem, other)

    def give_all(s):
        for i in every:
            for k in range(len(parts_of_sum(s, i))):
                give(s, i, k).start()

    def send_sum(s, i, k=None):
        layers, part = whole[i][0] if k is None else parts_of_sum(s, i)[k]
        source, place = (ref[i].at[s, span(*layers), span(*part)] for ref in (mine, partial))
        return remote(source, place, ring_out.at[i], hop_sem.at[s % chips, i], onward)

    def new_block(s, i, k, came):
        layers, part = parts_of_new(s - 1 if came else s, i)[k]
        return new[i].at[span(*layers), rows(i, device_at(-s, core), part)]

    def send_new(s, i, k):
        block = new_block(s, i, k, False)
        sem = end_sem.at[k] if len(parts_of_new(s, i)) > 1 else hop_sem.at[(last + s) % chips, i]
        return remote(block, block, ring_out.at[i], sem, onward)

    def forward(s, i, k):
        block = new_block(s, i, k, s > 0)
        return remote(block, block, chip_out.at[i], fwd_in.at[i], other)

    def load(i):
        return [
            pltpu.make_async_copy(weights[i].at[:, rows(i, me)], own_w[i], load_sem.at[i]),
            pltpu.make_async_copy(m_from[i], m_in[i], load_sem.at[i]),
            pltpu.make_async_copy(v_from[i], v_in[i], load_sem.at[i]),
        ]

    barrier = pltpu.get_barrier_semaphore()
    for device in (other, onward, device_at(-1, core)):
        pl.semaphore_signal(barrier, inc=1, device_id={"dp": device}, device_id_type=MESH)
    for i in every:
        fetch(0, i).start()
    pl.semaphore_wait(barrier, 3)
    give_all(0)
    for s in range(1, AHEAD):
        for i in every:
            fetch(s, i).start()
        give_all(s)

    def over_tiles(i, layers, part, do):
        for l in range(*layers):

            @pl.loop(part[0] // TILE, part[1] // TILE)
            def _(tile):
                do(i, l, tile, pl.ds(pl.multiple_of(tile * TILE, TILE), TILE))

    def total(s, i, l, at):
        g = mine[i][s, l, at].astype(jnp.float32) + theirs[i][s, l, at].astype(jnp.float32)
        if s > 0:
            g = g + partial[i][s - 1, l, at].astype(jnp.float32)
        return g.astype(jnp.bfloat16)

    for s in range(last):
        for i in every:
            fetch(s, i).wait()
            if s > 0:
                send_sum(s - 1, i).wait_recv()
            for k, (layers, part) in enumerate(parts_of_sum(s, i)):
                give(s, i, k).wait_recv()

                def add(i, l, tile, at):
                    mine[i][s, l, at] = total(s, i, l, at)

                over_tiles(i, layers, part, add)
                send_sum(s, i, k).start()
        if s + AHEAD < chips:
            for i in every:
                fetch(s + AHEAD, i).start()
            give_all(s + AHEAD)
        if s == 0:
            for i in every:
                for copy in load(i):
                    copy.start()

    for i in every:
        five = pl.ds(0, 5 * height[i])
        pltpu.make_async_copy(terms[i].at[0, :, five], new[i].at[:, five], load_sem.at[i]).wait()
        fetch(last, i).wait()
        give(last, i, 0).wait_recv()
        send_sum(last - 1, i).wait_recv()
        start = pl.multiple_of(me * height[i], TILE)

        def take_step(i, l, tile, at):
            g = total(last, i, l, at).astype(jnp.float32)
            w, m, v = adamw(own_w[i][l, at].astype(jnp.float32), m_in[i][l, at], v_in[i][l, at], g)
            new[i][l, pl.ds(pl.multiple_of(start + tile * TILE, TILE), TILE)] = w
            m_out[i][l, at] = m
            v_out[i][l, at] = v

        over_tiles(i, *whole[i][0], take_step)
        send_new(0, i, 0).start()
        forward(0, i, 0).start()
    for s in range(1, chips):
        for i in every:
            came = parts_of_new(s - 1, i)
            for k in range(len(came)):
                send_new(s - 1, i, k).wait_recv()
                if s < last and k == 0:
                    for q in range(len(parts_of_new(s, i))):
                        send_new(s, i, q).start()
                forward(s, i, k).start()
    for i in every:
        ring = new[i].at[:, pl.ds(0, 2 * last * height[i])]
        remote(ring, ring, ring_out.at[i], fwd_in.at[i], onward).wait_send()
        remote(new[i], new[i], chip_out.at[i], fwd_in.at[i], other).wait_send()
        half = new[i].at[:, pl.ds(0, chips * height[i])]
        remote(half, half, chip_out.at[i], fwd_in.at[i], other).wait_recv()


def solution(mesh):
    n = mesh.shape["dp"]
    chips = n // CORES

    def step(*arrays):
        terms, weights, m, v = (arrays[i : i + 3] for i in (0, 3, 6, 9))
        blocks = [one.shape for one in m]
        count = len(blocks)
        dma = pltpu.SemaphoreType.DMA

        def body(*refs):
            parts = [refs[i : i + 3] for i in range(0, 39, 3)]
            kernel(n, *parts, refs[39:])

        per_step = [pltpu.VMEM((chips, *shape), jnp.bfloat16) for shape in blocks]
        hops = [pltpu.VMEM((chips - 1, *shape), jnp.bfloat16) for shape in blocks]
        block = [pltpu.VMEM(shape, jnp.bfloat16) for shape in blocks]
        moments = [pltpu.VMEM(shape, jnp.float32) for shape in blocks]
        scratch = [*per_step, *per_step, *hops, *block, *moments, *moments]
        one = dma((count,))
        semaphores = [
            dma((AHEAD, count)),
            dma((2 * AHEAD, count)),
            dma((len(FIRST) + 2,)),
            dma((chips, count)),
            dma((len(LAST) + 2,)),
            *[one] * 4,
        ]
        hbm, vmem = pl.BlockSpec(memory_space=pltpu.HBM), pl.BlockSpec(memory_space=pltpu.VMEM)
        shapes = [jax.ShapeDtypeStruct(w.shape, w.dtype) for w in weights] + [jax.ShapeDtypeStruct(b, jnp.float32) for b in blocks] * 2
        inside = pl.pallas_call(
            body,
            out_shape=[pltpu.VMEM(one.shape, one.dtype) for one in shapes],
            in_specs=[hbm] * len(arrays),
            out_specs=[vmem] * len(shapes),
            scratch_shapes=[*scratch, *semaphores],
            compiler_params=pltpu.CompilerParams(collective_id=0, has_side_effects=True, vmem_limit_bytes=SCRATCH_BYTES),
        )(*arrays)
        return pl.pallas_call(
            functools.partial(write_out, len(shapes)),
            out_shape=shapes,
            in_specs=[vmem] * len(shapes),
            out_specs=[hbm] * len(shapes),
            scratch_shapes=[dma((len(shapes),))],
            compiler_params=pltpu.CompilerParams(vmem_limit_bytes=WRITE_BYTES),
        )(*inside)

    all_of, shared = P(None, None, None), P(None, "dp", None)
    return jax.shard_map(
        step,
        mesh=mesh,
        in_specs=(P(("rep", "dp"), None, None, None),) * 3 + (all_of,) * 3 + (shared,) * 6,
        out_specs=(P("rep", None, None),) * 3 + (P("rep", "dp", None),) * 6,
        check_vma=False,
    )
```

time: 347 us -> 176 us (0.51)
  waiting for transfers between devices: 313 us -> 0 us
  Pallas kernels: 0 us -> 175 us
  between operations: 14.2 us -> 0.65 us
  local copies, waits for them, and re-layouts: 12.3 us -> 0 us
  other arithmetic: 7.5 us -> 0 us
    reduce_scatter x3 -> x0, waiting for transfers between devices: 186 us -> none  [step(): lax.psum_scatter(t[0], 'dp', scatter_dimension=1, tiled=True)]
    pallas_call x0 -> x2, Pallas kernels: none -> 175 us  [the longest x1 168 us: step(): pl.pallas_call(body, out_shape=[pltpu.VMEM(one.shape, one.dtype) for one...]
    all_gather x3 -> x0, waiting for transfers between devices: 125 us -> none  [step(): whole = [lax.all_gather(one[0], 'dp', axis=1, tiled=True) for one in new]]
    unnamed x19 -> x0, local copies, waits for them, and re-layouts: 12.3 us -> none
    convert_element_type x3 -> x0, other arithmetic: 7.5 us -> none  [adamw(): return ((w - 0.02 * step).astype(jnp.bfloat16), m, v)]
  transfers between devices with their start and end apart: 6 -> 0, of which waited for: 6 -> 0; matrix products, arithmetic and copies ran while one was open for 2% -> 0% of each run, Pallas kernels for 0% -> 0%
where the time goes in v5:
time: 176 us; the launch traced here: 175 us
  Pallas kernels  175 us (99%)
    pallas_call x1, Pallas kernels, step(): pl.pallas_call(body, out_shape=[pltpu.VMEM(one.shape, one.dtype) for one...  168 us
    pallas_call x1, Pallas kernels, step(): pl.pallas_call(functools.partial(write_out, len(shapes)), out_shape=shape...  7.09 us

profile of v5, /device:TPU:21, one launch (start us, length us, event | category | flops | bytes accessed | tf_op | source)
XLA Modules:
  0.0 175.4 jit_solution(8024990438844700590)
XLA Ops:
  0.6 167.7 %shard_map.187 = (bf16[2,768,1792]{2,1,0:T(8,128)(2,1)S(1)}, bf16[2,768,1792]{2,1,0:T(8,128)(2,1)S(1)}, bf16[2,1792,768]{2,1,0:T(8,128)(2,1)S(1)}, f32[2,48,1792...) custom-call(bf16[1,2,768,1792]{3,2,1,0:T(8,128)(2,1)} %refs_0_.1, ...), custom_call_target="tpu_custom_call" | custom-call | tf_op jit(solution)/shard_map/pallas_call | solution.py:240
  168.3 7.1 %shard_map.188 = (bf16[2,768,1792]{2,1,0:T(8,128)(2,1)}, bf16[2,768,1792]{2,1,0:T(8,128)(2,1)}, bf16[2,1792,768]{2,1,0:T(8,128)(2,1)}, f32[2,48,1792]{2,1,0:T(8,...) custom-call(bf16[2,768,1792]{2,1,0:T(8,128)(2,1)S(1)} %get-tuple-ele, ...), custom_call_target="tpu_custom_call" | custom-call | tf_op jit(solution)/shard_map/pallas_call | solution.py:248

commit v6 on v0

v6 whole, which is shorter than its diff:
```python
import functools

import jax
import jax.numpy as jnp
from jax import lax
from jax.experimental import pallas as pl
from jax.experimental.pallas import tpu as pltpu
from jax.sharding import PartitionSpec as P

MESH = pl.DeviceIdType.MESH
CORES = 2
AHEAD = 1
FIRST = (1,)
LAST = (3,)
TILE = 16
SCRATCH_BYTES = 43 << 20
WRITE_BYTES = 1 << 20


def adamw(w, m, v, g):
    m = 0.9 * m + 0.1 * g
    v = 0.95 * v + 0.05 * g * g
    step = m * lax.rsqrt(v + 1e-8) + 0.1 * w
    return (w - 0.02 * step).astype(jnp.bfloat16), m, v


def write_out(groups, layers, *refs):
    kinds, count = len(refs) // (len(groups) + sum(map(len, groups))), sum(map(len, groups))
    places, sem = refs[kinds * len(groups) : -1], refs[-1]
    copies = []
    for kind in range(kinds):
        for source, group in zip(refs[kind * len(groups) :], groups, strict=False):
            for k, i in enumerate(group):
                q = kind * count + i
                copies.append(pltpu.make_async_copy(source.at[pl.ds(k * layers, layers)], places[q], sem.at[q]))
    for copy in copies:
        copy.start()
    for copy in copies:
        copy.wait()


def cut(shape, sizes, backwards):
    layers, height = shape[:2]
    ends, at = [], 0
    for size in sizes:
        ends.append((at, at + size * TILE))
        at += size * TILE
    ends.append((at, height))
    if backwards:
        ends = [(height - high, height - low) for low, high in reversed(ends)]
        return [((0, layers - 1), (0, height)), *[((layers - 1, layers), one) for one in ends]]
    return [*[((0, 1), one) for one in ends], *[((l, l + 1), (0, height)) for l in range(1, layers)]]


def kernel(n, groups, layers, terms, weights, m_from, v_from, new, m_out, v_out, mine, theirs, partial, own_w, m_in, v_in, sems):
    mine_sem, take_sem, first_sem, hop_sem, end_sem, load_sem, chip_out, ring_out, fwd_in = sems
    chips = n // CORES
    last = chips - 1
    me = lax.axis_index("dp")
    chip, core = me // CORES, me % CORES
    way = 1 - CORES * core
    other = chip * CORES + (1 - core)
    shapes = [ref.shape[1:] for ref in mine]
    height = [shape[1] for shape in shapes]
    every = range(len(groups))
    whole = [[((0, shape[0]), (0, shape[1]))] for shape in shapes]
    first, opening, final = [*whole], [*whole], [*whole]
    first[0] = cut(shapes[0], FIRST, False)
    opening[0] = [((l, l + layers), (0, height[0])) for l in range(0, shapes[0][0], layers)]
    final[-1] = cut(shapes[-1], LAST, True)

    def device_at(steps, which):
        return lax.rem(chip + way * steps + chips, chips) * CORES + which

    onward, across = device_at(1, core), device_at(1, 1 - core)

    def remote(source, place, send_sem, recv_sem, device):
        return pltpu.make_async_remote_copy(
            src_ref=source, dst_ref=place, send_sem=send_sem, recv_sem=recv_sem, device_id={"dp": device}, device_id_type=MESH
        )

    def rows(g, device, part=None):
        low, high = part or (0, height[g])
        return pl.ds(pl.multiple_of(device * height[g] + low, TILE), high - low)

    def span(low, high):
        return pl.ds(low, high - low)

    def by_array(g, part):
        low, high = part[0]
        for k, i in enumerate(groups[g]):
            a, b = max(low, k * layers), min(high, (k + 1) * layers)
            if a < b:
                yield i, pl.ds(a - k * layers, b - a), pl.ds(a, b - a)

    def fetch(s, g):
        for i, inner, outer in by_array(g, whole[g][0]):
            source = terms[i].at[0, inner, rows(g, device_at(-1 - s, core))]
            pltpu.make_async_copy(source, mine[g].at[s, outer], mine_sem.at[s % AHEAD, g]).start()

    def fetched(s, g):
        pltpu.make_async_copy(mine[g].at[s], mine[g].at[s], mine_sem.at[s % AHEAD, g]).wait()

    def parts_of_sum(s, g):
        return first[g] if s == 0 else whole[g]

    def parts_of_new(s, g):
        return final[g] if s == last - 1 else opening[g] if s == 0 else whole[g]

    def take_at(s, g, k):
        return first_sem.at[k] if len(parts_of_sum(s, g)) > 1 else take_sem.at[s % (2 * AHEAD), g]

    def give(s):
        for g in every:
            for k, part in enumerate(parts_of_sum(s, g)):
                for i, inner, outer in by_array(g, part):
                    source = terms[i].at[0, inner, rows(g, device_at(1 + s, 1 - core), part[1])]
                    remote(source, theirs[g].at[s, outer, span(*part[1])], chip_out.at[g], take_at(s, g, k), other).start()

    def taken(s, g, k):
        piece, part = parts_of_sum(s, g)[k]
        place = theirs[g].at[s, span(*piece), span(*part)]
        remote(place, place, chip_out.at[g], take_at(s, g, k), other).wait_recv()

    def send_sum(s, g, k=None):
        piece, part = whole[g][0] if k is None else parts_of_sum(s, g)[k]
        source, place = (ref[g].at[s, span(*piece), span(*part)] for ref in (mine, partial))
        return remote(source, place, ring_out.at[g], hop_sem.at[s % chips, g], onward)

    def is_end(s, g, k):
        return s == last - 1 and g == every[-1] and k == len(final[g]) - 1

    def send_new(s, g, k=None):
        piece, part = whole[g][0] if k is None else parts_of_new(s, g)[k]
        block = new[g].at[span(*piece), rows(g, device_at(-s, core), part)]
        sem = end_sem.at[k] if s == last - 1 and len(final[g]) > 1 else hop_sem.at[(last + s) % chips, g]
        return remote(block, block, ring_out.at[g], sem, onward)

    def hand(s, g, k):
        send_new(s, g, k).start()
        if is_end(s, g, k):
            piece, part = parts_of_new(s, g)[k]
            block = new[g].at[span(*piece), rows(g, device_at(-s, core), part)]
            remote(block, block, chip_out.at[g], fwd_in.at[g], across).start()

    def forward(s, g, part):
        block = new[g].at[span(*part[0]), rows(g, device_at(-s, core), part[1])]
        remote(block, block, chip_out.at[g], fwd_in.at[g], other).start()

    barrier = pltpu.get_barrier_semaphore()
    near = (other, onward, device_at(-1, core), across)
    for device in near:
        pl.semaphore_signal(barrier, inc=1, device_id={"dp": device}, device_id_type=MESH)
    for g in every:
        fetch(0, g)
    pl.semaphore_wait(barrier, len(near))
    give(0)
    for s in range(1, AHEAD):
        for g in every:
            fetch(s, g)
        give(s)

    def over_tiles(g, part, do):
        for l in range(*part[0]):

            @pl.loop(part[1][0] // TILE, part[1][1] // TILE)
            def _(tile):
                do(g, l, tile, pl.ds(pl.multiple_of(tile * TILE, TILE), TILE))

    def total(s, g, l, at):
        one = mine[g][s, l, at].astype(jnp.float32) + theirs[g][s, l, at].astype(jnp.float32)
        if s > 0:
            one = one + partial[g][s - 1, l, at].astype(jnp.float32)
        return one.astype(jnp.bfloat16)

    for s in range(last):
        for g in every:
            fetched(s, g)
            if s > 0:
                send_sum(s - 1, g).wait_recv()
            for k, part in enumerate(parts_of_sum(s, g)):
                taken(s, g, k)

                def add(g, l, tile, at):
                    mine[g][s, l, at] = total(s, g, l, at)

                over_tiles(g, part, add)
                send_sum(s, g, k).start()
        if s + AHEAD < chips:
            for g in every:
                fetch(s + AHEAD, g)
            give(s + AHEAD)
        if s == 0:
            for g in every:
                for i, _, outer in by_array(g, whole[g][0]):
                    pltpu.make_async_copy(weights[i].at[:, rows(g, me)], own_w[g].at[outer], load_sem.at[g]).start()
                    pltpu.make_async_copy(m_from[i], m_in[g].at[outer], load_sem.at[g]).start()
                    pltpu.make_async_copy(v_from[i], v_in[g].at[outer], load_sem.at[g]).start()

    for g in every:
        five = theirs[g].at[pl.ds(0, 5)]
        pltpu.make_async_copy(five, five, load_sem.at[g]).wait()
        fetched(last, g)
        taken(last, g, 0)
        send_sum(last - 1, g).wait_recv()
        start = pl.multiple_of(me * height[g], TILE)

        def take_step(g, l, tile, at):
            one = total(last, g, l, at).astype(jnp.float32)
            w, m, v = adamw(own_w[g][l, at].astype(jnp.float32), m_in[g][l, at], v_in[g][l, at], one)
            new[g][l, pl.ds(pl.multiple_of(start + tile * TILE, TILE), TILE)] = w
            m_out[g][l, at] = m
            v_out[g][l, at] = v

        for k, part in enumerate(parts_of_new(0, g)):
            over_tiles(g, part, take_step)
            hand(0, g, k)
            forward(0, g, part)
    for s in range(1, chips):
        for g in every:
            came = parts_of_new(s - 1, g)
            if s == last and len(came) > 1:
                for k, part in enumerate(came):
                    send_new(s - 1, g, k).wait_recv()
                    if not is_end(s - 1, g, k):
                        forward(s, g, part)
                continue
            send_new(s - 1, g).wait_recv()
            if s < last:
                for k in range(len(parts_of_new(s, g))):
                    hand(s, g, k)
            forward(s, g, whole[g][0])
    for g in every:
        ring = new[g].at[:, pl.ds(0, 2 * last * height[g])]
        remote(ring, ring, ring_out.at[g], fwd_in.at[g], onward).wait_send()
        remote(new[g], new[g], chip_out.at[g], fwd_in.at[g], other).wait_send()
        half = new[g].at[:, pl.ds(0, chips * height[g])]
        remote(half, half, chip_out.at[g], fwd_in.at[g], other).wait_recv()


def solution(mesh):
    n = mesh.shape["dp"]
    chips = n // CORES

    def step(*arrays):
        terms, weights, m, v = (arrays[i : i + 3] for i in (0, 3, 6, 9))
        blocks = [one.shape for one in m]
        layers = blocks[0][0]
        groups = [[i for i, b in enumerate(blocks) if b == shape] for shape in dict.fromkeys(blocks)]
        count, kinds = len(groups), (terms, weights, m, v)
        inputs = sum(map(len, kinds))
        dma = pltpu.SemaphoreType.DMA

        def body(*refs):
            given = [refs[i : i + len(m)] for i in range(0, inputs, len(m))]
            made = [refs[i : i + count] for i in range(inputs, inputs + 9 * count, count)]
            kernel(n, groups, layers, *given, *made, refs[inputs + 9 * count :])

        block = [(layers * len(group), *blocks[group[0]][1:]) for group in groups]
        full = [(layers * len(group), *weights[group[0]].shape[1:]) for group in groups]
        per_step = [pltpu.VMEM((chips, *one), jnp.bfloat16) for one in block]
        hops = [pltpu.VMEM((chips - 1, *one), jnp.bfloat16) for one in block]
        moments = [pltpu.VMEM(one, jnp.float32) for one in block]
        scratch = [*per_step, *per_step, *hops, *(pltpu.VMEM(one, jnp.bfloat16) for one in block), *moments, *moments]
        one = dma((count,))
        semaphores = [
            dma((AHEAD, count)),
            dma((2 * AHEAD, count)),
            dma((len(FIRST) + block[0][0],)),
            dma((chips, count)),
            dma((len(LAST) + 2,)),
            *[one] * 4,
        ]
        hbm, vmem = pl.BlockSpec(memory_space=pltpu.HBM), pl.BlockSpec(memory_space=pltpu.VMEM)
        inside = pl.pallas_call(
            body,
            out_shape=[*(pltpu.VMEM(one, jnp.bfloat16) for one in full), *moments, *moments],
            in_specs=[hbm] * len(arrays),
            out_specs=[vmem] * (3 * count),
            scratch_shapes=[*scratch, *semaphores],
            compiler_params=pltpu.CompilerParams(collective_id=0, has_side_effects=True, vmem_limit_bytes=SCRATCH_BYTES),
        )(*arrays)
        shapes = [jax.ShapeDtypeStruct(w.shape, w.dtype) for w in weights] + [jax.ShapeDtypeStruct(b, jnp.float32) for b in blocks] * 2
        return pl.pallas_call(
            functools.partial(write_out, groups, layers),
            out_shape=shapes,
            in_specs=[vmem] * (3 * count),
            out_specs=[hbm] * len(shapes),
            scratch_shapes=[dma((len(shapes),))],
            compiler_params=pltpu.CompilerParams(vmem_limit_bytes=WRITE_BYTES),
        )(*inside)

    all_of, shared = P(None, None, None), P(None, "dp", None)
    return jax.shard_map(
        step,
        mesh=mesh,
        in_specs=(P(("rep", "dp"), None, None, None),) * 3 + (all_of,) * 3 + (shared,) * 6,
        out_specs=(P("rep", None, None),) * 3 + (P("rep", "dp", None),) * 6,
        check_vma=False,
    )
```

time: 347 us -> 175 us (0.50)
  waiting for transfers between devices: 313 us -> 0 us
  Pallas kernels: 0 us -> 174 us
  between operations: 14.2 us -> 0.65 us
  local copies, waits for them, and re-layouts: 12.3 us -> 0 us
  other arithmetic: 7.5 us -> 0 us
    reduce_scatter x3 -> x0, waiting for transfers between devices: 186 us -> none  [step(): lax.psum_scatter(t[0], 'dp', scatter_dimension=1, tiled=True)]
    pallas_call x0 -> x2, Pallas kernels: none -> 174 us  [the longest x1 167 us: step(): pl.pallas_call(body, out_shape=[*(pltpu.VMEM(one, jnp.bfloat16) for one i...]
    all_gather x3 -> x0, waiting for transfers between devices: 125 us -> none  [step(): whole = [lax.all_gather(one[0], 'dp', axis=1, tiled=True) for one in new]]
    unnamed x19 -> x0, local copies, waits for them, and re-layouts: 12.3 us -> none
    convert_element_type x3 -> x0, other arithmetic: 7.5 us -> none  [adamw(): return ((w - 0.02 * step).astype(jnp.bfloat16), m, v)]
  transfers between devices with their start and end apart: 6 -> 0, of which waited for: 6 -> 0; matrix products, arithmetic and copies ran while one was open for 2% -> 0% of each run, Pallas kernels for 0% -> 0%
where the time goes in v6:
time: 175 us
  Pallas kernels  174 us (99%)
    pallas_call x1, Pallas kernels, step(): pl.pallas_call(body, out_shape=[*(pltpu.VMEM(one, jnp.bfloat16) for one i...  167 us
    pallas_call x1, Pallas kernels, step(): pl.pallas_call(functools.partial(write_out, groups, layers), out_shape=sh...  7.09 us

profile of v6, /device:TPU:21, one launch (start us, length us, event | category | flops | bytes accessed | tf_op | source)
XLA Modules:
  0.0 175.1 jit_solution(15037339697067246156)
XLA Ops:
  0.6 167.4 %shard_map.187 = (bf16[4,768,1792]{2,1,0:T(8,128)(2,1)S(1)}, bf16[2,1792,768]{2,1,0:T(8,128)(2,1)S(1)}, f32[4,48,1792]{2,1,0:T(8,128)S(1)}, f32[2,112,768]{2,1,0...) custom-call(bf16[1,2,768,1792]{3,2,1,0:T(8,128)(2,1)} %refs_0_.1, ...), custom_call_target="tpu_custom_call" | custom-call | tf_op jit(solution)/shard_map/pallas_call | solution.py:275
  168.0 7.1 %shard_map.188 = (bf16[2,768,1792]{2,1,0:T(8,128)(2,1)}, bf16[2,768,1792]{2,1,0:T(8,128)(2,1)}, bf16[2,1792,768]{2,1,0:T(8,128)(2,1)}, f32[2,48,1792]{2,1,0:T(8,...) custom-call(bf16[4,768,1792]{2,1,0:T(8,128)(2,1)S(1)} %get-tuple-ele, ...), custom_call_target="tpu_custom_call" | custom-call | tf_op jit(solution)/shard_map/pallas_call | solution.py:284

commit v7 on v6

--- a/solution.py
+++ b/solution.py
@@ -58,7 +58,7 @@
     last = chips - 1
     me = lax.axis_index("dp")
     chip, core = me // CORES, me % CORES
-    way = 1 - CORES * core
+    way = CORES * core - 1
     other = chip * CORES + (1 - core)
     shapes = [ref.shape[1:] for ref in mine]
     height = [shape[1] for shape in shapes]

time: 175 us -> 174 us (level)
  no operation moved by 1% of the time
where the time goes in v7:
time: 174 us
  Pallas kernels  173 us (99%)
    pallas_call x1, Pallas kernels, step(): pl.pallas_call(body, out_shape=[*(pltpu.VMEM(one, jnp.bfloat16) for one i...  166 us
    pallas_call x1, Pallas kernels, step(): pl.pallas_call(functools.partial(write_out, groups, layers), out_shape=sh...  7.09 us

profile of v7, /device:TPU:21, one launch (start us, length us, event | category | flops | bytes accessed | tf_op | source)
XLA Modules:
  0.0 174.1 jit_solution(11134048840039344541)
XLA Ops:
  0.6 166.4 %shard_map.187 = (bf16[4,768,1792]{2,1,0:T(8,128)(2,1)S(1)}, bf16[2,1792,768]{2,1,0:T(8,128)(2,1)S(1)}, f32[4,48,1792]{2,1,0:T(8,128)S(1)}, f32[2,112,768]{2,1,0...) custom-call(bf16[1,2,768,1792]{3,2,1,0:T(8,128)(2,1)} %refs_0_.1, ...), custom_call_target="tpu_custom_call" | custom-call | tf_op jit(solution)/shard_map/pallas_call | solution.py:275
  167.1 7.1 %shard_map.188 = (bf16[2,768,1792]{2,1,0:T(8,128)(2,1)}, bf16[2,768,1792]{2,1,0:T(8,128)(2,1)}, bf16[2,1792,768]{2,1,0:T(8,128)(2,1)}, f32[2,48,1792]{2,1,0:T(8,...) custom-call(bf16[4,768,1792]{2,1,0:T(8,128)(2,1)S(1)} %get-tuple-ele, ...), custom_call_target="tpu_custom_call" | custom-call | tf_op jit(solution)/shard_map/pallas_call | solution.py:284

commit v8 on v7

--- a/solution.py
+++ b/solution.py
@@ -11,7 +11,7 @@
 CORES = 2
 AHEAD = 1
 FIRST = (1,)
-LAST = (3,)
+LAST = (3, 3)
 TILE = 16
 SCRATCH_BYTES = 43 << 20
 WRITE_BYTES = 1 << 20
@@ -27,16 +27,13 @@
 def write_out(groups, layers, *refs):
     kinds, count = len(refs) // (len(groups) + sum(map(len, groups))), sum(map(len, groups))
     places, sem = refs[kinds * len(groups) : -1], refs[-1]
-    copies = []
     for kind in range(kinds):
-        for source, group in zip(refs[kind * len(groups) :], groups, strict=False):
+        for g, group in enumerate(groups):
+            a = kind * len(groups) + g
             for k, i in enumerate(group):
-                q = kind * count + i
-                copies.append(pltpu.make_async_copy(source.at[pl.ds(k * layers, layers)], places[q], sem.at[q]))
-    for copy in copies:
-        copy.start()
-    for copy in copies:
-        copy.wait()
+                pltpu.make_async_copy(refs[a].at[pl.ds(k * layers, layers)], places[kind * count + i], sem.at[a]).start()
+    for a in range(kinds * len(groups)):
+        pltpu.make_async_copy(refs[a], refs[a], sem.at[a]).wait()
 
 
 def cut(shape, sizes, backwards):
@@ -49,7 +46,7 @@
     if backwards:
         ends = [(height - high, height - low) for low, high in reversed(ends)]
         return [((0, layers - 1), (0, height)), *[((layers - 1, layers), one) for one in ends]]
-    return [*[((0, 1), one) for one in ends], *[((l, l + 1), (0, height)) for l in range(1, layers)]]
+    return [*[((0, 1), one) for one in ends], ((1, layers), (0, height))]
 
 
 def kernel(n, groups, layers, terms, weights, m_from, v_from, new, m_out, v_out, mine, theirs, partial, own_w, m_in, v_in, sems):
@@ -148,7 +145,7 @@
         remote(block, block, chip_out.at[g], fwd_in.at[g], other).start()
 
     barrier = pltpu.get_barrier_semaphore()
-    near = (other, onward, device_at(-1, core), across)
+    near = (onward, device_at(-1, core), across, other)
     for device in near:
         pl.semaphore_signal(barrier, inc=1, device_id={"dp": device}, device_id_type=MESH)
     for g in every:
@@ -266,7 +263,7 @@
         semaphores = [
             dma((AHEAD, count)),
             dma((2 * AHEAD, count)),
-            dma((len(FIRST) + block[0][0],)),
+            dma((len(FIRST) + 2,)),
             dma((chips, count)),
             dma((len(LAST) + 2,)),
             *[one] * 4,
@@ -286,7 +283,7 @@
             out_shape=shapes,
             in_specs=[vmem] * (3 * count),
             out_specs=[hbm] * len(shapes),
-            scratch_shapes=[dma((len(shapes),))],
+            scratch_shapes=[dma((3 * count,))],
             compiler_params=pltpu.CompilerParams(vmem_limit_bytes=WRITE_BYTES),
         )(*inside)
 

time: 174 us -> 174 us (level)
  no operation moved by 1% of the time
where the time goes in v8:
time: 174 us
  Pallas kernels  173 us (99%)
    pallas_call x1, Pallas kernels, step(): pl.pallas_call(body, out_shape=[*(pltpu.VMEM(one, jnp.bfloat16) for one i...  166 us
    pallas_call x1, Pallas kernels, step(): pl.pallas_call(functools.partial(write_out, groups, layers), out_shape=sh...  7.06 us

profile of v8, /device:TPU:21, one launch (start us, length us, event | category | flops | bytes accessed | tf_op | source)
XLA Modules:
  0.0 174.1 jit_solution(6898357786594346250)
XLA Ops:
  0.6 166.3 %shard_map.187 = (bf16[4,768,1792]{2,1,0:T(8,128)(2,1)S(1)}, bf16[2,1792,768]{2,1,0:T(8,128)(2,1)S(1)}, f32[4,48,1792]{2,1,0:T(8,128)S(1)}, f32[2,112,768]{2,1,0...) custom-call(bf16[1,2,768,1792]{3,2,1,0:T(8,128)(2,1)} %refs_0_.1, ...), custom_call_target="tpu_custom_call" | custom-call | tf_op jit(solution)/shard_map/pallas_call | solution.py:272
  167.0 7.1 %shard_map.188 = (bf16[2,768,1792]{2,1,0:T(8,128)(2,1)}, bf16[2,768,1792]{2,1,0:T(8,128)(2,1)}, bf16[2,1792,768]{2,1,0:T(8,128)(2,1)}, f32[2,48,1792]{2,1,0:T(8,...) custom-call(bf16[4,768,1792]{2,1,0:T(8,128)(2,1)S(1)} %get-tuple-ele, ...), custom_call_target="tpu_custom_call" | custom-call | tf_op jit(solution)/shard_map/pallas_call | solution.py:281

commit v9 on v8

--- a/solution.py
+++ b/solution.py
@@ -50,7 +50,8 @@
 
 
 def kernel(n, groups, layers, terms, weights, m_from, v_from, new, m_out, v_out, mine, theirs, partial, own_w, m_in, v_in, sems):
-    mine_sem, take_sem, first_sem, hop_sem, end_sem, load_sem, chip_out, ring_out, fwd_in = sems
+    mine_sem, take_sem, first_sem, hop_sem, end_sem, chip_out, ring_out, fwd_in = sems
+    load_sem = first_sem
     chips = n // CORES
     last = chips - 1
     me = lax.axis_index("dp")
@@ -266,7 +267,7 @@
             dma((len(FIRST) + 2,)),
             dma((chips, count)),
             dma((len(LAST) + 2,)),
-            *[one] * 4,
+            *[one] * 3,
         ]
         hbm, vmem = pl.BlockSpec(memory_space=pltpu.HBM), pl.BlockSpec(memory_space=pltpu.VMEM)
         inside = pl.pallas_call(

time: 174 us -> 174 us (level)
  no operation moved by 1% of the time
where the time goes in v9:
time: 174 us
  Pallas kernels  173 us (99%)
    pallas_call x1, Pallas kernels, step(): pl.pallas_call(body, out_shape=[*(pltpu.VMEM(one, jnp.bfloat16) for one i...  166 us
    pallas_call x1, Pallas kernels, step(): pl.pallas_call(functools.partial(write_out, groups, layers), out_shape=sh...  7.06 us

profile of v9, /device:TPU:21, one launch (start us, length us, event | category | flops | bytes accessed | tf_op | source)
XLA Modules:
  0.0 174.0 jit_solution(7639592320276905395)
XLA Ops:
  0.6 166.3 %shard_map.187 = (bf16[4,768,1792]{2,1,0:T(8,128)(2,1)S(1)}, bf16[2,1792,768]{2,1,0:T(8,128)(2,1)S(1)}, f32[4,48,1792]{2,1,0:T(8,128)S(1)}, f32[2,112,768]{2,1,0...) custom-call(bf16[1,2,768,1792]{3,2,1,0:T(8,128)(2,1)} %refs_0_.1, ...), custom_call_target="tpu_custom_call" | custom-call | tf_op jit(solution)/shard_map/pallas_call | solution.py:273
  167.0 7.1 %shard_map.188 = (bf16[2,768,1792]{2,1,0:T(8,128)(2,1)}, bf16[2,768,1792]{2,1,0:T(8,128)(2,1)}, bf16[2,1792,768]{2,1,0:T(8,128)(2,1)}, f32[2,48,1792]{2,1,0:T(8,...) custom-call(bf16[4,768,1792]{2,1,0:T(8,128)(2,1)S(1)} %get-tuple-ele, ...), custom_call_target="tpu_custom_call" | custom-call | tf_op jit(solution)/shard_map/pallas_call | solution.py:282
